TPU v7x, 32 devices: a 4x4x1 block of a 4x4x8 slice. The times are simulated.
32 devices in a mesh: rep: 1 (over z), col: 4 (over y), row: 8 (over x, core).
Axes of the slice: x: 4, y: 4, z: 1, core: 2. Of those that a mesh axis runs over, the one named last changes fastest.
The devices are a block of a 4x4x8 slice.
Arguments:
- hidden_0: bfloat16 [128, 2048], P('rep', 'row')
- hidden_1: bfloat16 [128, 2048], P('rep', 'row')
- positions: int32 [128], P(('rep', 'row'))
- lengths: int32 [128], P(('rep', 'row'))
- cache_k: bfloat16 [2, 128, 1024, 8, 64], P(None, ('rep', 'row'), None, 'col')
- cache_v: bfloat16 [2, 128, 1024, 8, 64], P(None, ('rep', 'row'), None, 'col')
- norm_attn: bfloat16 [2, 2048], P(None, 'row')
- norm_mlp: bfloat16 [2, 2048], P(None, 'row')
- w_query: bfloat16 [2, 2048, 2048], P(None, 'row', 'col')
- w_key: bfloat16 [2, 2048, 512], P(None, 'row', 'col')
- w_value: bfloat16 [2, 2048, 512], P(None, 'row', 'col')
- w_out: bfloat16 [2, 2048, 2048], P(None, 'row', 'col')
- w_gate: bfloat16 [2, 2048, 8192], P(None, 'row', 'col')
- w_up: bfloat16 [2, 2048, 8192], P(None, 'row', 'col')
- w_down: bfloat16 [2, 8192, 2048], P(None, 'row', 'col')
Outputs:
- output 1: bfloat16 [128, 2048], P('rep', 'row')
- output 2: bfloat16 [128, 2048], P('rep', 'row')
- output 3: bfloat16 [2, 128, 1024, 8, 64], P(None, ('rep', 'row'), None, 'col')
- output 4: bfloat16 [2, 128, 1024, 8, 64], P(None, ('rep', 'row'), None, 'col')
All inputs are finite; a program needn't handle non-finite values.
Results may differ from a plain program's by a relative error of at most 0.02.
Values are sent between devices in bfloat16 or wider.
A program may use at most 768 MiB of HBM per device.

v0:
```python
import jax
import jax.numpy as jnp
from jax import lax
from jax.sharding import PartitionSpec as P

ROPE_BASE = 1000000.0
EPS = 1e-05


def rope_rotate(vectors, positions):
    head_dim = vectors.shape[-1]
    half = head_dim // 2
    inv_freq = jnp.power(jnp.float32(ROPE_BASE), -jnp.arange(half, dtype=jnp.float32) * 2.0 / head_dim)
    angles = positions.astype(jnp.float32)[:, None, None] * inv_freq
    cosine = jnp.cos(angles)
    sine = jnp.sin(angles)
    vec_f32 = vectors.astype(jnp.float32)
    first = vec_f32[..., :half]
    second = vec_f32[..., half:]
    return jnp.concatenate([first * cosine - second * sine, second * cosine + first * sine], axis=-1).astype(jnp.bfloat16)


def add_residual(hidden, update):
    return (hidden.astype(jnp.float32) + update.astype(jnp.float32)).astype(jnp.bfloat16)


def attend_local(query, keys, vals, slots):
    scores = jnp.einsum('bkgd,blkd->bkgl', query, keys, preferred_element_type=jnp.float32) * (keys.shape[-1] ** -0.5)
    valid = jnp.arange(keys.shape[1])[None, None, None, :] <= slots[:, None, None, None]
    probs = jax.nn.softmax(jnp.where(valid, scores, -jnp.inf), axis=-1).astype(jnp.bfloat16)
    return jnp.einsum('bkgl,blkd->bkgd', probs, vals, preferred_element_type=jnp.float32).astype(jnp.bfloat16)


def solution(mesh):
    row_count = mesh.shape['row']
    hidden_spec = P('rep', 'row')
    index_spec = P(('rep', 'row'))
    cache_spec = P(None, ('rep', 'row'), None, 'col', None)
    gain_spec = P(None, 'row')
    weight_spec = P(None, 'row', 'col')

    def rms_norm(hidden, gain):
        hidden_f = hidden.astype(jnp.float32)
        square_sum = lax.psum(jnp.sum(hidden_f * hidden_f, axis=-1, keepdims=True), 'row')
        scale = lax.rsqrt(square_sum / (hidden.shape[-1] * row_count) + EPS)
        return (hidden_f * scale * gain.astype(jnp.float32)).astype(jnp.bfloat16)

    def sum_rows(partial):
        return lax.psum_scatter(partial.astype(jnp.bfloat16), 'row', scatter_dimension=0, tiled=True)

    def to_row_features(block):
        whole = lax.all_gather(block, 'col', axis=1, tiled=True)
        return lax.all_to_all(whole, 'row', 1, 0, tiled=True)

    def decoder_layer(hidden, layer, cache_k, cache_v, positions, slots, weights):
        norm_attn, norm_mlp, w_query, w_key, w_value, w_out, w_gate, w_up, w_down = weights
        head_dim = cache_k.shape[-1]
        kv_local = cache_k.shape[-2]
        q_local = w_query.shape[-1]
        kv_cols = w_key.shape[-1]
        ff_local = w_gate.shape[-1]
        normed = rms_norm(hidden, norm_attn[layer])
        qkv_part = jnp.concatenate([
            jnp.dot(normed, w_query[layer], preferred_element_type=jnp.float32),
            jnp.dot(normed, w_key[layer], preferred_element_type=jnp.float32),
            jnp.dot(normed, w_value[layer], preferred_element_type=jnp.float32)], axis=1)
        qkv_local = sum_rows(qkv_part)
        batch_local = qkv_local.shape[0]
        query = rope_rotate(qkv_local[:, :q_local].reshape(batch_local, -1, head_dim), positions)
        key_new = rope_rotate(qkv_local[:, q_local:q_local + kv_cols].reshape(batch_local, kv_local, head_dim), positions)
        value_new = qkv_local[:, q_local + kv_cols:].reshape(batch_local, kv_local, head_dim)
        rows = jnp.arange(batch_local)
        cache_k = cache_k.at[layer, rows, slots].set(key_new)
        cache_v = cache_v.at[layer, rows, slots].set(value_new)
        attended = attend_local(query.reshape(batch_local, kv_local, -1, head_dim), cache_k[layer], cache_v[layer], slots)
        attn_rows = to_row_features(attended.reshape(batch_local, -1))
        attn_out = to_row_features(sum_rows(jnp.dot(attn_rows, w_out[layer], preferred_element_type=jnp.float32)))
        hidden = add_residual(hidden, attn_out)
        normed = rms_norm(hidden, norm_mlp[layer])
        gate_up = sum_rows(jnp.concatenate([
            jnp.dot(normed, w_gate[layer], preferred_element_type=jnp.float32),
            jnp.dot(normed, w_up[layer], preferred_element_type=jnp.float32)], axis=1))
        activated = (jax.nn.silu(gate_up[:, :ff_local].astype(jnp.float32)) * gate_up[:, ff_local:].astype(jnp.float32)).astype(jnp.bfloat16)
        down_out = to_row_features(sum_rows(jnp.dot(to_row_features(activated), w_down[layer], preferred_element_type=jnp.float32)))
        return add_residual(hidden, down_out), cache_k, cache_v

    def device_program(hidden_0, hidden_1, positions, lengths, cache_k, cache_v, norm_attn, norm_mlp, w_query, w_key, w_value, w_out, w_gate, w_up, w_down):
        weights = (norm_attn, norm_mlp, w_query, w_key, w_value, w_out, w_gate, w_up, w_down)
        outputs = []
        for step, hidden in enumerate((hidden_0, hidden_1)):
            for layer in range(w_query.shape[0]):
                hidden, cache_k, cache_v = decoder_layer(hidden, layer, cache_k, cache_v, positions + step, lengths + step, weights)
            outputs.append(hidden)
        return outputs[0], outputs[1], cache_k, cache_v

    return jax.shard_map(device_program, mesh=mesh,
                         in_specs=(hidden_spec, hidden_spec, index_spec, index_spec, cache_spec, cache_spec, gain_spec, gain_spec) + (weight_spec,) * 7,
                         out_specs=(hidden_spec, hidden_spec, cache_spec, cache_spec), check_vma=False)
```

profile of v0, /device:TPU:97, one launch (start us, length us, event | category | flops | bytes accessed | tf_op | source)
XLA Modules:
  0.0 1155.6 jit_solution(7626050046248696556)
XLA Ops:
  9.0 13.9 %psum.56 = f32[128,1]{0,1:T(1,128)S(1)} all-reduce(f32[128,1]{0,1:T(1,128)S(1)} %bitcast.408), channel_id=1, replica_groups=mesh['rep'=1,'col'=4,'row'=8] {'row'}, use_global_device_ids=true, to_apply=%region_1.0 | all-reduce | flops 128 | bytes 1024 | tf_op jit(solution)/shard_map/psum | solution.py:44
  28.5 39.5 %copy.120 = bf16[2,16,1024,2,64]{4,3,2,1,0:T(2,128)(2,1)} copy(bf16[2,16,1024,2,64]{2,4,3,1,0:T(8,128)(2,1)} %param.20) | data formatting | bytes 16777216 | tf_op args[5]
  68.0 39.5 %copy.118 = bf16[2,16,1024,2,64]{4,3,2,1,0:T(2,128)(2,1)} copy(bf16[2,16,1024,2,64]{2,4,3,1,0:T(8,128)(2,1)} %param.19) | data formatting | bytes 16777216 | tf_op args[4]
  119.1 20.0 %copy.161 = bf16[1,16,1024,2,64]{2,4,3,1,0:T(8,128)(2,1)} copy(bf16[1,16,1024,2,64]{4,3,2,1,0:T(2,128)(2,1)} %slice.298) | data formatting | bytes 8388608
  149.8 20.1 %copy.160 = bf16[1,16,1024,2,64]{2,4,3,1,0:T(8,128)(2,1)} copy(bf16[1,16,1024,2,64]{4,3,2,1,0:T(2,128)(2,1)} %slice.296) | data formatting | bytes 8388608
  187.6 13.1 %all_to_all.256 = bf16[16,8,256]{2,0,1:T(8,128)(2,1)S(1)} all-to-all(bf16[16,8,256]{2,0,1:T(8,128)(2,1)S(1)} %bitcast.374), channel_id=1, replica_groups=mesh['rep'=1,'col'=4,'row'=8] {'row'}, dimensions={1} | all-to-all | bytes 131072 | tf_op jit(solution)/shard_map/all_to_all | solution.py:53
  201.5 25.0 %reduce-scatter.19.cloned.1.call-done = bf16[16,512]{1,0:T(8,128)(2,1)} async-done(((bf16[128,512]{1,0:T(8,128)(2,1)}), bf16[16,512]{1,0:T(8,128)(2,1)}) %reduce-scatter.19.cloned.1.call-update) | async-done | bytes 16400 | tf_op jit(solution)/shard_map/reduce_scatter | solution.py:49
  250.9 12.6 %psum.57 = f32[128,1]{0,1:T(1,128)S(1)} all-reduce(f32[128,1]{0,1:T(1,128)S(1)} %bitcast.405), channel_id=1, replica_groups=mesh['rep'=1,'col'=4,'row'=8] {'row'}, use_global_device_ids=true, to_apply=%region_9.10 | all-reduce | flops 128 | bytes 1024 | tf_op jit(solution)/shard_map/psum | solution.py:44
  266.7 25.4 %reduce-scatter.21.cloned.1.call-done = bf16[16,4096]{1,0:T(8,128)(2,1)} async-done(((bf16[128,4096]{1,0:T(8,128)(2,1)}), bf16[16,4096]{1,0:T(8,128)(2,1)}) %reduce-scatter.21.cloned.1.call-update) | async-done | bytes 131088 | tf_op jit(solution)/shard_map/reduce_scatter | solution.py:49
  303.2 15.1 %all_to_all.257 = bf16[16,8,1024]{2,0,1:T(8,128)(2,1)S(1)} all-to-all(bf16[16,8,1024]{2,0,1:T(8,128)(2,1)S(1)} %bitcast.352), channel_id=1, replica_groups=mesh['rep'=1,'col'=4,'row'=8] {'row'}, dimensions={1} | all-to-all | bytes 524288 | tf_op jit(solution)/shard_map/all_to_all | solution.py:53
  321.3 24.1 %reduce-scatter.23.cloned.1.call-done = bf16[16,512]{1,0:T(8,128)(2,1)} async-done(((bf16[128,512]{1,0:T(8,128)(2,1)}), bf16[16,512]{1,0:T(8,128)(2,1)}) %reduce-scatter.23.cloned.1.call-update) | async-done | bytes 16400 | tf_op jit(solution)/shard_map/reduce_scatter | solution.py:49
  369.7 13.1 %all-reduce.1 = (f32[128,1]{0,1:T(1,128)S(1)}, f32[128,1]{0,1:T(1,128)}) all-reduce(f32[128,1]{0,1:T(1,128)S(1)} %bitcast.406, f32[128,1]{0,1:T(1,128)S(1)} %bitcast.403), channel_id=1, replica_groups=mesh['rep'=1,'col'=4,'row'=8] {'row'}, use_global_device_ids=true, to_apply=%region_13.14 | all-reduce | flops 256 | bytes 2048 | tf_op jit(solution)/shard_map/psum | solution.py:44
  390.9 19.3 %reduce-scatter.25.cloned.1.call-done = bf16[16,768]{1,0:T(8,128)(2,1)} async-done(((bf16[128,768]{1,0:T(8,128)(2,1)}), bf16[16,768]{1,0:T(8,128)(2,1)}) %reduce-scatter.25.cloned.1.call-update) | async-done | bytes 24592 | tf_op jit(solution)/shard_map/reduce_scatter | solution.py:49
  450.7 20.1 %copy.165 = bf16[1,16,1024,2,64]{2,4,3,1,0:T(8,128)(2,1)} copy(bf16[1,16,1024,2,64]{4,3,2,1,0:T(2,128)(2,1)} %slice.320) | data formatting | bytes 8388608
  481.7 20.2 %copy.164 = bf16[1,16,1024,2,64]{2,4,3,1,0:T(8,128)(2,1)} copy(bf16[1,16,1024,2,64]{4,3,2,1,0:T(2,128)(2,1)} %slice.318) | data formatting | bytes 8388608
  518.5 13.2 %all_to_all.258 = bf16[16,8,256]{2,0,1:T(8,128)(2,1)S(1)} all-to-all(bf16[16,8,256]{2,0,1:T(8,128)(2,1)S(1)} %bitcast.375), channel_id=1, replica_groups=mesh['rep'=1,'col'=4,'row'=8] {'row'}, dimensions={1} | all-to-all | bytes 131072 | tf_op jit(solution)/shard_map/all_to_all | solution.py:53
  532.7 24.4 %reduce-scatter.35.cloned.1.call-done = bf16[16,512]{1,0:T(8,128)(2,1)} async-done(((bf16[128,512]{1,0:T(8,128)(2,1)}), bf16[16,512]{1,0:T(8,128)(2,1)}) %reduce-scatter.35.cloned.1.call-update) | async-done | bytes 16400 | tf_op jit(solution)/shard_map/reduce_scatter | solution.py:49
  566.7 13.2 %all_to_all.259 = bf16[16,8,256]{2,0,1:T(8,128)(2,1)S(1)} all-to-all(bf16[16,8,256]{2,0,1:T(8,128)(2,1)S(1)} %bitcast.376), channel_id=1, replica_groups=mesh['rep'=1,'col'=4,'row'=8] {'row'}, dimensions={1} | all-to-all | bytes 131072 | tf_op jit(solution)/shard_map/all_to_all | solution.py:53
  580.1 12.6 %psum.61 = f32[128,1]{0,1:T(1,128)S(1)} all-reduce(f32[128,1]{0,1:T(1,128)S(1)} %bitcast.407), channel_id=1, replica_groups=mesh['rep'=1,'col'=4,'row'=8] {'row'}, use_global_device_ids=true, to_apply=%region_33.34 | all-reduce | flops 128 | bytes 1024 | tf_op jit(solution)/shard_map/psum | solution.py:44
  596.5 25.5 %reduce-scatter.37.cloned.1.call-done = bf16[16,4096]{1,0:T(8,128)(2,1)} async-done(((bf16[128,4096]{1,0:T(8,128)(2,1)}), bf16[16,4096]{1,0:T(8,128)(2,1)}) %reduce-scatter.37.cloned.1.call-update) | async-done | bytes 131088 | tf_op jit(solution)/shard_map/reduce_scatter | solution.py:49
  633.0 15.1 %all_to_all.260 = bf16[16,8,1024]{2,0,1:T(8,128)(2,1)S(1)} all-to-all(bf16[16,8,1024]{2,0,1:T(8,128)(2,1)S(1)} %bitcast.353), channel_id=1, replica_groups=mesh['rep'=1,'col'=4,'row'=8] {'row'}, dimensions={1} | all-to-all | bytes 524288 | tf_op jit(solution)/shard_map/all_to_all | solution.py:53
  650.4 24.8 %reduce-scatter.39.cloned.1.call-done = bf16[16,512]{1,0:T(8,128)(2,1)} async-done(((bf16[128,512]{1,0:T(8,128)(2,1)}), bf16[16,512]{1,0:T(8,128)(2,1)}) %reduce-scatter.39.cloned.1.call-update) | async-done | bytes 16400 | tf_op jit(solution)/shard_map/reduce_scatter | solution.py:49
  684.9 13.5 %all_to_all.261 = bf16[16,8,256]{2,0,1:T(8,128)(2,1)S(1)} all-to-all(bf16[16,8,256]{2,0,1:T(8,128)(2,1)S(1)} %bitcast.377), channel_id=1, replica_groups=mesh['rep'=1,'col'=4,'row'=8] {'row'}, dimensions={1} | all-to-all | bytes 131072 | tf_op jit(solution)/shard_map/all_to_all | solution.py:53
  698.5 12.6 %psum.62 = f32[128,1]{0,1:T(1,128)S(1)} all-reduce(f32[128,1]{0,1:T(1,128)S(1)} %bitcast.409), channel_id=1, replica_groups=mesh['rep'=1,'col'=4,'row'=8] {'row'}, use_global_device_ids=true, to_apply=%region_37.38 | all-reduce | flops 128 | bytes 1024 | tf_op jit(solution)/shard_map/psum | solution.py:44
  714.2 20.1 %copy.163 = bf16[1,16,1024,2,64]{2,4,3,1,0:T(8,128)(2,1)} copy(bf16[1,16,1024,2,64]{4,3,2,1,0:T(2,128)(2,1)} %slice.309) | data formatting | bytes 8388608
  734.3 20.1 %copy.162 = bf16[1,16,1024,2,64]{2,4,3,1,0:T(8,128)(2,1)} copy(bf16[1,16,1024,2,64]{4,3,2,1,0:T(2,128)(2,1)} %slice.307) | data formatting | bytes 8388608
  783.0 38.8 %copy.145 = bf16[2,16,1024,2,64]{2,4,3,1,0:T(8,128)(2,1)} copy(bf16[2,16,1024,2,64]{4,3,2,1,0:T(2,128)(2,1)} %scatter_fusion.7) | data formatting | bytes 16777216 | tf_op jit(solution)/shard_map/scatter | solution.py:74
  824.6 38.9 %copy.144 = bf16[2,16,1024,2,64]{2,4,3,1,0:T(8,128)(2,1)} copy(bf16[2,16,1024,2,64]{4,3,2,1,0:T(2,128)(2,1)} %scatter_fusion.6) | data formatting | bytes 16777216 | tf_op jit(solution)/shard_map/scatter | solution.py:73
  894.1 23.5 %reduce-scatter.27.cloned.1.call-done = bf16[16,512]{1,0:T(8,128)(2,1)} async-done(((bf16[128,512]{1,0:T(8,128)(2,1)}), bf16[16,512]{1,0:T(8,128)(2,1)}) %reduce-scatter.27.cloned.1.call-update) | async-done | bytes 16400 | tf_op jit(solution)/shard_map/reduce_scatter | solution.py:49
  971.3 12.6 %all-reduce = (f32[128,1]{0,1:T(1,128)S(1)}, f32[128,1]{0,1:T(1,128)S(1)}) all-reduce(f32[128,1]{0,1:T(1,128)S(1)} %bitcast.402, f32[128,1]{0,1:T(1,128)S(1)} %bitcast.404), channel_id=1, replica_groups=mesh['rep'=1,'col'=4,'row'=8] {'row'}, use_global_device_ids=true, to_apply=%region_21.22 | all-reduce | flops 256 | bytes 2048 | tf_op jit(solution)/shard_map/psum | solution.py:44
  990.5 22.1 %reduce-scatter.29.cloned.1.call-done = bf16[16,4096]{1,0:T(8,128)(2,1)} async-done(((bf16[128,4096]{1,0:T(8,128)(2,1)}), bf16[16,4096]{1,0:T(8,128)(2,1)}) %reduce-scatter.29.cloned.1.call-update) | async-done | bytes 131088 | tf_op jit(solution)/shard_map/reduce_scatter | solution.py:49
  1074.6 19.8 %reduce-scatter.31.cloned.1.call-done = bf16[16,512]{1,0:T(8,128)(2,1)} async-done(((bf16[128,512]{1,0:T(8,128)(2,1)}), bf16[16,512]{1,0:T(8,128)(2,1)}) %reduce-scatter.31.cloned.1.call-update) | async-done | bytes 16400 | tf_op jit(solution)/shard_map/reduce_scatter | solution.py:49
  (274 shorter events, 468.9 us)
Async XLA Ops:
  7.2 100.6 %reduce-scatter.17.cloned.1.call-start = ((), (), s32[]{:S(2)}) async-start(), calls=%async_computation.32 | async-start | bytes 221184 | tf_op jit(solution)/shard_map/reduce_scatter | solution.py:49
  8.0 374.8 %copy-start.23 = (f32[1,256]{1,0:T(1,128)}, f32[1,256]{1,0:T(1,128)S(1)}, u32[]{:S(2)}) copy-start(f32[1,256]{1,0:T(1,128)S(1)} %get-tuple-element.58) | copy-start | bytes 3076
  27.0 199.6 %reduce-scatter.19.cloned.1.call-start = ((), (), s32[]{:S(2)}) async-start(), calls=%async_computation.33 | async-start | bytes 147456 | tf_op jit(solution)/shard_map/reduce_scatter | solution.py:49
  28.5 141.7 %copy-start.14 = (pred[16,1024]{1,0:T(8,128)(4,1)}, pred[16,1024]{1,0:T(8,128)(4,1)S(1)}, u32[]{:S(2)}) copy-start(pred[16,1024]{1,0:T(8,128)(4,1)S(1)} %iota_compare_fusion.1) | copy-start | bytes 49156
  107.7 313.9 %copy-start.10 = (f32[16,32]{1,0:T(8,128)}, f32[16,32]{1,0:T(8,128)S(1)}, u32[]{:S(2)}) copy-start(f32[16,32]{1,0:T(8,128)S(1)} %get-tuple-element.60) | copy-start | bytes 6148
  107.7 313.9 %copy-start.12 = (f32[16,32]{1,0:T(8,128)}, f32[16,32]{1,0:T(8,128)S(1)}, u32[]{:S(2)}) copy-start(f32[16,32]{1,0:T(8,128)S(1)} %get-tuple-element.61) | copy-start | bytes 6148
  107.7 394.3 %copy-start.7 = (f32[16,32]{1,0:T(8,128)}, f32[16,32]{1,0:T(8,128)S(1)}, u32[]{:S(2)}) copy-start(f32[16,32]{1,0:T(8,128)S(1)} %get-tuple-element.53) | copy-start | bytes 6148
  236.9 13.9 %all-to-all-start.1 = ((bf16[16,8,256]{2,0,1:T(8,128)(2,1)}), bf16[16,8,256]{2,0,1:T(8,128)(2,1)S(1)}, u32[]{:S(2)}, u32[]{:S(2)}) async-start(bf16[16,8,256]{2,0,1:T(8,128)(2,1)} %bitcast.346), calls=%async_computation.3 | async-start | bytes 131072 | tf_op jit(solution)/shard_map/all_to_all | solution.py:53
  246.1 46.1 %reduce-scatter.21.cloned.1.call-start = ((), (), s32[]{:S(2)}) async-start(), calls=%async_computation.34 | async-start | bytes 1179648 | tf_op jit(solution)/shard_map/reduce_scatter | solution.py:49
  266.7 78.7 %reduce-scatter.23.cloned.1.call-start = ((), (), s32[]{:S(2)}) async-start(), calls=%async_computation.35 | async-start | bytes 147456 | tf_op jit(solution)/shard_map/reduce_scatter | solution.py:49
  355.6 14.0 %all-to-all-start.3 = ((bf16[16,8,256]{2,0,1:T(8,128)(2,1)}), bf16[16,8,256]{2,0,1:T(8,128)(2,1)S(1)}, u32[]{:S(2)}, u32[]{:S(2)}) async-start(bf16[16,8,256]{2,0,1:T(8,128)(2,1)} %bitcast.345), calls=%async_computation.7 | async-start | bytes 131072 | tf_op jit(solution)/shard_map/all_to_all | solution.py:53
  364.9 45.2 %reduce-scatter.25.cloned.1.call-start = ((), (), s32[]{:S(2)}) async-start(), calls=%async_computation.36 | async-start | bytes 221184 | tf_op jit(solution)/shard_map/reduce_scatter | solution.py:49
  385.9 53.5 %reduce-scatter.33.cloned.1.call-start = ((), (), s32[]{:S(2)}) async-start(), calls=%async_computation.40 | async-start | bytes 221184 | tf_op jit(solution)/shard_map/reduce_scatter | solution.py:49
  390.6 166.4 %reduce-scatter.35.cloned.1.call-start = ((), (), s32[]{:S(2)}) async-start(), calls=%async_computation.41 | async-start | bytes 147456 | tf_op jit(solution)/shard_map/reduce_scatter | solution.py:49
  532.6 89.4 %reduce-scatter.37.cloned.1.call-start = ((), (), s32[]{:S(2)}) async-start(), calls=%async_computation.42 | async-start | bytes 1179648 | tf_op jit(solution)/shard_map/reduce_scatter | solution.py:49
  593.7 119.5 %copy-start.3 = (bf16[2,256,512]{2,1,0:T(8,128)(2,1)S(1)}, bf16[2,256,512]{2,1,0:T(8,128)(2,1)}, u32[]{:S(2)}) copy-start(bf16[2,256,512]{2,1,0:T(8,128)(2,1)} %param.23) | copy-start | bytes 1572868
  596.5 78.8 %reduce-scatter.39.cloned.1.call-start = ((), (), s32[]{:S(2)}) async-start(), calls=%async_computation.43 | async-start | bytes 147456 | tf_op jit(solution)/shard_map/reduce_scatter | solution.py:49
  650.4 104.1 %reduce-scatter.41.cloned.1.call-start = ((), (), s32[]{:S(2)}) async-start(), calls=%async_computation.44 | async-start | bytes 221184 | tf_op jit(solution)/shard_map/reduce_scatter | solution.py:49
  772.8 108.0 %all-to-all-start.4 = ((bf16[16,8,256]{2,0,1:T(8,128)(2,1)}), bf16[16,8,256]{2,0,1:T(8,128)(2,1)S(1)}, u32[]{:S(2)}, u32[]{:S(2)}) async-start(bf16[16,8,256]{2,0,1:T(8,128)(2,1)} %bitcast.344), calls=%async_computation.9 | async-start | bytes 131072 | tf_op jit(solution)/shard_map/all_to_all | solution.py:53
  880.8 12.4 %all-to-all-start.12 = ((bf16[16,8,256]{2,0,1:T(8,128)(2,1)}), bf16[16,8,256]{2,0,1:T(8,128)(2,1)S(1)}, u32[]{:S(2)}, u32[]{:S(2)}) async-start(bf16[16,8,256]{2,0,1:T(8,128)(2,1)} %bitcast.338), calls=%async_computation.25 | async-start | bytes 131072 | tf_op jit(solution)/shard_map/all_to_all | solution.py:53
  888.5 29.0 %reduce-scatter.27.cloned.1.call-start = ((), (), s32[]{:S(2)}) async-start(), calls=%async_computation.37 | async-start | bytes 147456 | tf_op jit(solution)/shard_map/reduce_scatter | solution.py:49
  889.4 57.5 %reduce-scatter.43.cloned.1.call-start = ((), (), s32[]{:S(2)}) async-start(), calls=%async_computation.45 | async-start | bytes 147456 | tf_op jit(solution)/shard_map/reduce_scatter | solution.py:49
  927.9 29.2 %all-to-all-start.5 = ((bf16[16,8,256]{2,0,1:T(8,128)(2,1)}), bf16[16,8,256]{2,0,1:T(8,128)(2,1)S(1)}, u32[]{:S(2)}, u32[]{:S(2)}) async-start(bf16[16,8,256]{2,0,1:T(8,128)(2,1)} %bitcast.343), calls=%async_computation.11 | async-start | bytes 131072 | tf_op jit(solution)/shard_map/all_to_all | solution.py:53
  957.1 14.1 %all-to-all-start.13 = ((bf16[16,8,256]{2,0,1:T(8,128)(2,1)}), bf16[16,8,256]{2,0,1:T(8,128)(2,1)S(1)}, u32[]{:S(2)}, u32[]{:S(2)}) async-start(bf16[16,8,256]{2,0,1:T(8,128)(2,1)} %bitcast.337), calls=%async_computation.27 | async-start | bytes 131072 | tf_op jit(solution)/shard_map/all_to_all | solution.py:53
  966.5 46.1 %reduce-scatter.29.cloned.1.call-start = ((), (), s32[]{:S(2)}) async-start(), calls=%async_computation.38 | async-start | bytes 1179648 | tf_op jit(solution)/shard_map/reduce_scatter | solution.py:49
  987.1 58.0 %reduce-scatter.45.cloned.1.call-start = ((), (), s32[]{:S(2)}) async-start(), calls=%async_computation.46 | async-start | bytes 1179648 | tf_op jit(solution)/shard_map/reduce_scatter | solution.py:49
  1024.3 31.9 %all-to-all-start.6 = ((bf16[16,8,1024]{2,0,1:T(8,128)(2,1)}), bf16[16,8,1024]{2,0,1:T(8,128)(2,1)S(1)}, u32[]{:S(2)}, u32[]{:S(2)}) async-start(bf16[16,8,1024]{2,0,1:T(8,128)(2,1)} %bitcast.334), calls=%async_computation.13 | async-start | bytes 524288 | tf_op jit(solution)/shard_map/all_to_all | solution.py:53
  1056.3 16.1 %all-to-all-start.14 = ((bf16[16,8,1024]{2,0,1:T(8,128)(2,1)}), bf16[16,8,1024]{2,0,1:T(8,128)(2,1)S(1)}, u32[]{:S(2)}, u32[]{:S(2)}) async-start(bf16[16,8,1024]{2,0,1:T(8,128)(2,1)} %bitcast.332), calls=%async_computation.29 | async-start | bytes 524288 | tf_op jit(solution)/shard_map/all_to_all | solution.py:53
  1066.0 28.5 %reduce-scatter.31.cloned.1.call-start = ((), (), s32[]{:S(2)}) async-start(), calls=%async_computation.39 | async-start | bytes 147456 | tf_op jit(solution)/shard_map/reduce_scatter | solution.py:49
  1068.2 55.6 %reduce-scatter.47.cloned.1.call-start = ((), (), s32[]{:S(2)}) async-start(), calls=%async_computation.47 | async-start | bytes 147456 | tf_op jit(solution)/shard_map/reduce_scatter | solution.py:49
  1104.8 29.1 %all-to-all-start.7 = ((bf16[16,8,256]{2,0,1:T(8,128)(2,1)}), bf16[16,8,256]{2,0,1:T(8,128)(2,1)S(1)}, u32[]{:S(2)}, u32[]{:S(2)}) async-start(bf16[16,8,256]{2,0,1:T(8,128)(2,1)} %bitcast.342), calls=%async_computation.15 | async-start | bytes 131072 | tf_op jit(solution)/shard_map/all_to_all | solution.py:53
  1133.8 14.2 %all-to-all-start.15 = ((bf16[16,8,256]{2,0,1:T(8,128)(2,1)}), bf16[16,8,256]{2,0,1:T(8,128)(2,1)S(1)}, u32[]{:S(2)}, u32[]{:S(2)}) async-start(bf16[16,8,256]{2,0,1:T(8,128)(2,1)} %bitcast.336), calls=%async_computation.31 | async-start | bytes 131072 | tf_op jit(solution)/shard_map/all_to_all | solution.py:53
  (23 other events, 1210.3 us)
Sparse Core Ops, SparseCore 0:
  27.1 27.9 reduce-scatter.16
  201.7 24.8 reduce-scatter.18
  266.8 25.3 reduce-scatter.20
  320.7 24.6 reduce-scatter.22
  386.0 24.0 reduce-scatter.24
  412.2 27.0 reduce-scatter.32
  532.7 24.2 reduce-scatter.34
  596.6 25.4 reduce-scatter.36
  650.5 24.6 reduce-scatter.38
  714.3 24.1 reduce-scatter.40
  891.6 25.9 reduce-scatter.26
  919.7 27.2 reduce-scatter.42
  987.2 25.3 reduce-scatter.28
  1014.7 30.2 reduce-scatter.44
  1068.7 25.6 reduce-scatter.30
  1096.6 27.2 reduce-scatter.46
where the time goes:
time: 1170 us; the launch traced here: 1160 us
  local copies, waits for them, and re-layouts  354 us (30%)
  blocking collectives  316 us (27%)
  waiting for transfers between devices  298 us (25%)
  starting transfers between devices  90.8 us (8%)
  matrix products  58.9 us (5%)
  other arithmetic  22.8 us (2%)
  between operations  15 us (1%)
    reduce_scatter x16, waiting for transfers between devices, sum_rows(): lax.psum_scatter(partial.astype(jnp.bfloat16), 'row', scatter_dimension=0...  272 us
    unnamed x66, local copies, waits for them, and re-layouts  200 us
    all_gather x16, blocking collectives, to_row_features(): whole = lax.all_gather(block, 'col', axis=1, tiled=True)  155 us
    all_to_all x10, starting transfers between devices, to_row_features(): return lax.all_to_all(whole, 'row', 1, 0, tiled=True)  89.6 us
    all_to_all x6, blocking collectives, to_row_features(): return lax.all_to_all(whole, 'row', 1, 0, tiled=True)  83.1 us
    psum x6, blocking collectives, rms_norm(): lax.psum(jnp.sum(hidden_f * hidden_f, axis=-1, keepdims=True), 'row')  77.4 us
    scatter x5, local copies, waits for them, and re-layouts, decoder_layer(): cache_v = cache_v.at[layer, rows, slots].set(value_new)  49.2 us
    scatter x5, local copies, waits for them, and re-layouts, decoder_layer(): cache_k = cache_k.at[layer, rows, slots].set(key_new)  49.1 us
  transfers between devices with their start and end apart: 26, of which 20 were waited for; matrix products, arithmetic and copies ran while one was open for 22% of the time, Pallas kernels for 0%

commit v1 on v0

v1 whole, which is shorter than its diff:
```python
import functools

import jax
import jax.numpy as jnp
import numpy as np
from jax import lax
from jax.experimental import pallas as pl
from jax.experimental.pallas import tpu as pltpu
from jax.sharding import PartitionSpec as P

ROPE_BASE = 1000000.0
EPS = 1e-05
MESH = pl.DeviceIdType.MESH
BF16 = jnp.bfloat16
F32 = jnp.float32
STEPS = 2


def at_multiple(index, size):
    return pl.ds(pl.multiple_of(index * size, size), size)


def decode_kernel(
        h0, h1, pos, lens, kc, vc, gain_a, gain_m, freq, wq, wk, wv, wo, wg, wu, wd,
        out0, out1, new_kv,
        hin, gsrc, gful, kbuf, vbuf, wqkv, wov, wgu, wdv,
        xst, xmid, nst1, nin1, qs, qr, ob, oin, os_, orr, nst2, nin2, gs, gr, aa, ab, ds_, dr,
        qf, of, kn, vn, cs, sn,
        hin_sem, kv_sem, w_sem, wx_send, wx_recv, init_send, init_recv, g_send, g_recv,
        n1_send, n1_recv, q_send, q_recv, o_send, o_recv, ro_send, ro_recv, x_send, x_recv,
        n2_send, n2_recv, gu_send, gu_recv, aa_send, aa_recv, ab_send, ab_recv, rd_send, rd_recv,
        x2_send, x2_recv, out_sem):
    layers = wq.shape[0]
    rows_n = lax.axis_size('row')
    cols_n = lax.axis_size('col')
    chips_n = rows_n // 2
    r = lax.axis_index('row')
    c = lax.axis_index('col')
    chip, core = r // 2, r % 2
    batch, ks = h0.shape
    hb = batch // rows_n
    width = ks * rows_n
    cw = wo.shape[-1]
    q_w = wq.shape[-1]
    kv_w = wk.shape[-1]
    qkv_w = q_w + 2 * kv_w
    ff = wg.shape[-1]
    fh = ff // 2
    cb = batch // chips_n
    ctx = kc.shape[-1]
    hins = (h0, h1)
    outs = (out0, out1)

    def peer_copy(src, dst, send_sem, recv_sem, row, col):
        return pltpu.make_async_remote_copy(
            src_ref=src, dst_ref=dst, send_sem=send_sem, recv_sem=recv_sem,
            device_id={'row': row, 'col': col}, device_id_type=MESH)

    def wait_recv(ref, sem):
        peer_copy(ref, ref, sem, sem, r, c).wait_recv()

    def wait_send(ref, sem):
        peer_copy(ref, ref, sem, sem, r, c).wait_send()

    for s in range(STEPS):
        pltpu.make_async_copy(hins[s], hin.at[s], hin_sem.at[s]).start()
    for l in range(layers):
        for src, lo, n in ((wq, 0, q_w), (wk, q_w, kv_w), (wv, q_w + kv_w, kv_w)):
            pltpu.make_async_copy(src.at[l], wqkv.at[l, :, pl.ds(lo, n)], w_sem.at[l, 0]).start()
        pltpu.make_async_copy(kc.at[l], kbuf.at[l], kv_sem.at[l, 0]).start()
        pltpu.make_async_copy(vc.at[l], vbuf.at[l], kv_sem.at[l, 1]).start()
        pltpu.make_async_copy(wo.at[l], wov.at[l], w_sem.at[l, 1]).start()
        for k, src in enumerate((wg, wu)):
            pltpu.make_async_copy(src.at[l, :, at_multiple(core, fh)],
                                  wgu.at[l, at_multiple(core, ks), pl.ds(k * fh, fh)], w_sem.at[l, 2]).start()
        pltpu.make_async_copy(wd.at[l], wdv.at[l], w_sem.at[l, 3]).start()
    gsrc[...] = jnp.concatenate([gain_a[...].astype(F32), gain_m[...].astype(F32),
                                 jnp.zeros((gsrc.shape[0] - 2 * layers, ks), F32)], axis=0)
    gful[:, at_multiple(r, ks)] = gsrc[...]

    barrier = pltpu.get_barrier_semaphore()
    for k in range(1, rows_n * cols_n):
        other = lax.rem(r * cols_n + c + k, rows_n * cols_n)
        pl.semaphore_signal(barrier, inc=1, device_id={'row': other // cols_n, 'col': lax.rem(other, cols_n)},
                            device_id_type=MESH)
    pl.semaphore_wait(barrier, rows_n * cols_n - 1)

    def row_peer(d):
        return lax.rem(r + d, rows_n)

    for d in range(1, rows_n):
        peer_copy(gsrc, gful.at[:, at_multiple(r, ks)], g_send, g_recv, row_peer(d), c).start()
    for s in range(STEPS):
        pltpu.make_async_copy(hins[s], hin.at[s], hin_sem.at[s]).wait()
        for d in range(1, rows_n):
            peer_copy(hin.at[s, at_multiple(row_peer(d), hb), :], xst.at[0, s, :, at_multiple(r, ks)],
                      init_send.at[s], init_recv.at[s], row_peer(d), c).start()
        xst[0, s, :, at_multiple(r, ks)] = hin[s, at_multiple(r, hb), :]
    for l in range(layers):
        for k, src in enumerate((wg, wu)):
            peer_copy(src.at[l, :, at_multiple(1 - core, fh)],
                      wgu.at[l, at_multiple(core, ks), pl.ds(k * fh, fh)],
                      wx_send.at[l], wx_recv.at[l], r + 1 - 2 * core, c).start()

    lane = lax.broadcasted_iota(jnp.int32, (hb, 128), 1)
    sub = lax.broadcasted_iota(jnp.int32, (hb, 128), 0)
    first_half = lax.rem(lane, 64) < 32
    pos_col = jnp.zeros((hb, 128), jnp.int32)
    for b in range(hb):
        pos_col = jnp.where(sub == b, pos[b], pos_col)
    for s in range(STEPS):
        angle = (pos_col + s).astype(F32) * freq[...]
        cs[s] = jnp.cos(angle)
        sine = jnp.sin(angle)
        sn[s] = jnp.where(first_half, -sine, sine)

    def norm_rows(x, gain_row):
        xf = x.astype(F32)
        scale = lax.rsqrt(jnp.sum(xf * xf, axis=-1, keepdims=True) * (1.0 / width) + EPS)
        return (xf * scale * gful[pl.ds(gain_row, 1), :]).astype(BF16)

    def send_n1(l, s):
        for d in range(1, rows_n):
            peer_copy(nst1.at[l, s, :, at_multiple(row_peer(d), ks)], nin1.at[l, s, at_multiple(r, hb), :],
                      n1_send.at[l, s], n1_recv.at[l, s], row_peer(d), c).start()
        nin1[l, s, at_multiple(r, hb), :] = nst1[l, s, :, at_multiple(r, ks)]

    wait_recv(gful.at[:, pl.ds(0, (rows_n - 1) * ks)], g_recv)
    for s in range(STEPS):
        wait_recv(xst.at[0, s, :, pl.ds(0, (rows_n - 1) * ks)], init_recv.at[s])
        nst1[0, s] = norm_rows(xst[0, s], 0)
        send_n1(0, s)

    def reduce_rows(stage, recv, sem, l, s):
        wait_recv(recv.at[l, s], sem.at[l, s])
        total = stage[l, s, at_multiple(r, hb), :].astype(F32)
        for d in range(rows_n - 1):
            total += recv[l, s, d].astype(F32)
        return total

    def scatter_rows(stage, recv, send_sem, recv_sem, l, s):
        for d in range(1, rows_n):
            peer_copy(stage.at[l, s, at_multiple(row_peer(d), hb), :], recv.at[l, s, d - 1],
                      send_sem.at[l, s], recv_sem.at[l, s], row_peer(d), c).start()

    def rope(x, s):
        turned = jnp.where(first_half, pltpu.roll(x, 96, 1), pltpu.roll(x, 32, 1))
        return (x * cs[s] + turned * sn[s]).astype(BF16).astype(F32)

    def attention(l, s):
        qkv = reduce_rows(qs, qr, q_recv, l, s).astype(BF16).astype(F32)
        key = rope(qkv[:, q_w:q_w + kv_w], s)
        val = qkv[:, q_w + kv_w:]
        kn[s] = key
        vn[s] = val
        new_kv[l, s, 0] = key
        new_kv[l, s, 1] = val
        for t in range(4):
            kv, pair = t // 2, t % 2
            y = rope(qkv[:, 128 * t:128 * t + 128], s)
            for e in range(2):
                z = y if e == kv else pltpu.roll(y, 64, 1)
                qf[pl.ds(kv * 4 + pair * 2 + e, hb, stride=8), :] = jnp.where(lane // 64 == kv, z, 0.0)
        slot = lax.broadcasted_iota(jnp.int32, (8, ctx), 1)

        def group(gi, carry):
            for u in range(4):
                b = gi * 4 + u
                qv = qf[at_multiple(b, 8), :]
                sc = jnp.dot(qv.astype(BF16), kbuf[l, b], preferred_element_type=F32) * 0.125
                sc = jnp.where(slot < lens[b], sc, -jnp.inf)
                top = jnp.max(sc, axis=-1, keepdims=True)
                news = []
                for e in range(s + 1):
                    news.append(jnp.sum(qv * kn[e, pl.ds(b, 1), :], axis=-1, keepdims=True) * 0.125)
                    top = jnp.maximum(top, news[e])
                p = jnp.exp(sc - top)
                news = [jnp.exp(x - top) for x in news]
                inv = 1.0 / functools.reduce(lambda x, y: x + y, news, jnp.sum(p, axis=-1, keepdims=True))
                o = lax.dot_general((p * inv).astype(BF16), vbuf[l, b], (((1,), (1,)), ((), ())),
                                    preferred_element_type=F32)
                for e in range(s + 1):
                    o += (news[e] * inv).astype(BF16).astype(F32) * vn[e, pl.ds(b, 1), :]
                of[at_multiple(b, 8), :] = o
            return carry

        lax.fori_loop(0, hb // 4, group, 0)
        for t in range(4):
            kv, pair = t // 2, t % 2
            lo = of[pl.ds(kv * 4 + pair * 2, hb, stride=8), :]
            hi = of[pl.ds(kv * 4 + pair * 2 + 1, hb, stride=8), :]
            lo = lo if kv == 0 else pltpu.roll(lo, 64, 1)
            hi = hi if kv == 1 else pltpu.roll(hi, 64, 1)
            ob[l, s, :, 128 * t:128 * t + 128] = jnp.where(lane < 64, lo, hi).astype(BF16)
        for j in range(2):
            for d in range(cols_n):
                copy = peer_copy(ob.at[l, s, :, pl.ds(j * ks, ks)], oin.at[l, s, at_multiple(r, hb), :],
                                 o_send.at[l, s], o_recv.at[l, s], 2 * c + j, lax.rem(c + d, cols_n))
                if d == 0:
                    mine = r == 2 * c + j

                    @pl.when(mine)
                    def _():
                        oin[l, s, at_multiple(r, hb), :] = ob[l, s, :, pl.ds(j * ks, ks)]

                    @pl.when(jnp.logical_not(mine))
                    def _():
                        copy.start()
                else:
                    copy.start()

    def on_own_column(full, short, wait, sem):
        @pl.when(chip == c)
        def _():
            wait(short, sem)

        @pl.when(chip != c)
        def _():
            wait(full, sem)

    def add_block(x, update):
        block = x[:, at_multiple(c, cw)].astype(F32)
        return (block + update.astype(BF16).astype(F32)).astype(BF16)

    def gather_cols(dst, block, send_sem, recv_sem):
        dst[:, at_multiple(c, cw)] = block
        for d in range(1, cols_n):
            peer_copy(dst.at[:, at_multiple(c, cw)], dst.at[:, at_multiple(c, cw)], send_sem, recv_sem,
                      r, lax.rem(c + d, cols_n)).start()

    def layer(l, carry):
        for s in range(STEPS):
            if s == 0:
                for src, lo, n in ((wq, 0, q_w), (wk, q_w, kv_w), (wv, q_w + kv_w, kv_w)):
                    pltpu.make_async_copy(src.at[l], wqkv.at[l, :, pl.ds(lo, n)], w_sem.at[l, 0]).wait()
            wait_recv(nin1.at[l, s, pl.ds(0, batch - hb), :], n1_recv.at[l, s])
            qs[l, s] = jnp.dot(nin1[l, s], wqkv[l], preferred_element_type=F32).astype(BF16)
            scatter_rows(qs, qr, q_send, q_recv, l, s)
        for s in range(STEPS):
            if s == 0:
                pltpu.make_async_copy(kc.at[l], kbuf.at[l], kv_sem.at[l, 0]).wait()
                pltpu.make_async_copy(vc.at[l], vbuf.at[l], kv_sem.at[l, 1]).wait()
            attention(l, s)
        for s in range(STEPS):
            if s == 0:
                pltpu.make_async_copy(wo.at[l], wov.at[l], w_sem.at[l, 1]).wait()
            on_own_column(oin.at[l, s], oin.at[l, s, pl.ds(0, batch - hb), :], wait_recv, o_recv.at[l, s])
            os_[l, s] = jnp.dot(oin[l, s], wov[l], preferred_element_type=F32).astype(BF16)
            scatter_rows(os_, orr, ro_send, ro_recv, l, s)
        for s in range(STEPS):
            total = reduce_rows(os_, orr, ro_recv, l, s)
            gather_cols(xmid.at[l, s], add_block(xst.at[l, s], total), x_send.at[l, s], x_recv.at[l, s])
        for s in range(STEPS):
            wait_recv(xmid.at[l, s, :, pl.ds(0, width - cw)], x_recv.at[l, s])
            nst2[l, s] = norm_rows(xmid[l, s], layers + l)
            for d in range(1, rows_n):
                to = row_peer(d)
                peer_copy(nst2.at[l, s, :, at_multiple(to // 2, 2 * ks)], nin2.at[l, s, at_multiple(r, hb), :],
                          n2_send.at[l, s], n2_recv.at[l, s], to, c).start()
            nin2[l, s, at_multiple(r, hb), :] = nst2[l, s, :, at_multiple(chip, 2 * ks)]
        for s in range(STEPS):
            if s == 0:
                for k, src in enumerate((wg, wu)):
                    pltpu.make_async_copy(src.at[l, :, at_multiple(core, fh)],
                                          wgu.at[l, at_multiple(core, ks), pl.ds(k * fh, fh)], w_sem.at[l, 2]).wait()
                wait_recv(wgu.at[l, pl.ds(0, ks), :], wx_recv.at[l])
            wait_recv(nin2.at[l, s, pl.ds(0, batch - hb), :], n2_recv.at[l, s])
            tile = 512

            def columns(k, carry):
                gs[l, s, :, at_multiple(k, tile)] = jnp.dot(
                    nin2[l, s], wgu[l, :, at_multiple(k, tile)], preferred_element_type=F32).astype(BF16)
                return carry

            lax.fori_loop(0, 2 * fh // tile, columns, 0)
            for d in range(1, chips_n):
                to = lax.rem(chip + d, chips_n)
                peer_copy(gs.at[l, s, at_multiple(to, cb), :], gr.at[l, s, d - 1],
                          gu_send.at[l, s], gu_recv.at[l, s], 2 * to + core, c).start()
        for s in range(STEPS):
            wait_recv(gr.at[l, s], gu_recv.at[l, s])
            total = gs[l, s, at_multiple(chip, cb), :].astype(F32)
            for d in range(chips_n - 1):
                total += gr[l, s, d].astype(F32)
            total = total.astype(BF16).astype(F32)
            gate, up = total[:, :fh], total[:, fh:]
            aa[l, s, c] = (gate / (1.0 + jnp.exp(-gate)) * up).astype(BF16)
            for d in range(1, cols_n):
                peer_copy(aa.at[l, s, c], aa.at[l, s, c], aa_send.at[l, s], aa_recv.at[l, s, c],
                          r, lax.rem(c + d, cols_n)).start()
        for s in range(STEPS):
            for d in (1, 2, 3, 0):
                to = lax.rem(chip + d, chips_n)

                @pl.when(to != c)
                def _():
                    wait_recv(aa.at[l, s, to], aa_recv.at[l, s, to])

                if d:
                    peer_copy(aa.at[l, s, to], ab.at[l, s, at_multiple(chip, cb), :],
                              ab_send.at[l, s], ab_recv.at[l, s], 2 * to + core, c).start()
                else:
                    ab[l, s, at_multiple(chip, cb), :] = aa[l, s, to]
        for s in range(STEPS):
            if s == 0:
                pltpu.make_async_copy(wd.at[l], wdv.at[l], w_sem.at[l, 3]).wait()
            wait_recv(ab.at[l, s, pl.ds(0, batch - cb), :], ab_recv.at[l, s])
            ds_[l, s] = jnp.dot(ab[l, s], wdv[l], preferred_element_type=F32).astype(BF16)
            scatter_rows(ds_, dr, rd_send, rd_recv, l, s)
        for s in range(STEPS):
            total = reduce_rows(ds_, dr, rd_recv, l, s)
            gather_cols(xst.at[l + 1, s], add_block(xmid.at[l, s], total), x2_send.at[l, s], x2_recv.at[l, s])
        last = l == layers - 1
        for s in range(STEPS):
            wait_recv(xst.at[l + 1, s, :, pl.ds(0, width - cw)], x2_recv.at[l, s])
            x = xst[l + 1, s]
            nst1[l + 1, s] = jnp.where(last, x, norm_rows(x, jnp.minimum(l + 1, layers - 1)))
            send_n1(l + 1, s)
        return carry

    lax.fori_loop(0, layers, layer, 0)

    for s in range(STEPS):
        wait_recv(nin1.at[layers, s, pl.ds(0, batch - hb), :], n1_recv.at[layers, s])
        pltpu.make_async_copy(nin1.at[layers, s], outs[s], out_sem.at[s]).start()

    for d in range(1, rows_n):
        wait_send(gsrc, g_send)
    for s in range(STEPS):
        wait_send(hin.at[s, pl.ds(0, batch - hb), :], init_send.at[s])

    def finish(l, carry):
        wait_send(wgu.at[l, pl.ds(0, ks), :], wx_send.at[l])
        for s in range(STEPS):
            wait_send(nin1.at[l, s, pl.ds(0, batch - hb), :], n1_send.at[l, s])
            wait_send(qr.at[l, s], q_send.at[l, s])
            on_own_column(oin.at[l, s], oin.at[l, s, pl.ds(0, batch - hb), :], wait_send, o_send.at[l, s])
            wait_send(orr.at[l, s], ro_send.at[l, s])
            wait_send(xmid.at[l, s, :, pl.ds(0, width - cw)], x_send.at[l, s])
            wait_send(nin2.at[l, s, pl.ds(0, batch - hb), :], n2_send.at[l, s])
            wait_send(gr.at[l, s], gu_send.at[l, s])
            wait_send(aa.at[l, s, pl.ds(0, cols_n - 1)], aa_send.at[l, s])
            wait_send(ab.at[l, s, pl.ds(0, batch - cb), :], ab_send.at[l, s])
            wait_send(dr.at[l, s], rd_send.at[l, s])
            wait_send(xst.at[l + 1, s, :, pl.ds(0, width - cw)], x2_send.at[l, s])
        return carry

    lax.fori_loop(0, layers, finish, 0)
    for s in range(STEPS):
        wait_send(nin1.at[layers, s, pl.ds(0, batch - hb), :], n1_send.at[layers, s])
        pltpu.make_async_copy(nin1.at[layers, s], outs[s], out_sem.at[s]).wait()


def cache_kernel(lens, new_kv, kc, vc, ko, vo, buf, in_sem, out_sem):
    layers, seqs = kc.shape[0], kc.shape[1]
    caches, results = (kc, vc), (ko, vo)

    def load(i, carry):
        l, b = i // seqs, lax.rem(i, seqs)
        for w in range(2):
            pltpu.make_async_copy(caches[w].at[l, b], buf.at[w, i], in_sem.at[w, i]).start()
        return carry

    def store(i, carry):
        l, b = i // seqs, lax.rem(i, seqs)
        first = lens[b]
        rows = lax.broadcasted_iota(jnp.int32, (8, 128), 0)
        lane = lax.broadcasted_iota(jnp.int32, (kc.shape[2], 128), 1)
        for w in range(2):
            pltpu.make_async_copy(caches[w].at[l, b], buf.at[w, i], in_sem.at[w, i]).wait()
            for s in range(STEPS):
                row = jnp.broadcast_to(new_kv[l, s, w, pl.ds(b, 1), :], (8, 128))
                spread = lax.dot_general(jnp.where(rows == 0, row, 0.0).astype(BF16), jnp.ones((8, 128), BF16),
                                         (((0,), (0,)), ((), ())), preferred_element_type=F32)
                slot = first + s
                window = pl.ds(pl.multiple_of(slot // 128 * 128, 128), 128)
                old = buf[w, i, :, window].astype(F32)
                buf[w, i, :, window] = jnp.where(lane == lax.rem(slot, 128), spread, old).astype(BF16)
            pltpu.make_async_copy(buf.at[w, i], results[w].at[l, b], out_sem).start()
        return carry

    lax.fori_loop(0, layers * seqs, load, 0)
    lax.fori_loop(0, layers * seqs, store, 0)

    def drain(i, carry):
        l, b = i // seqs, lax.rem(i, seqs)
        for w in range(2):
            pltpu.make_async_copy(buf.at[w, i], results[w].at[l, b], out_sem).wait()
        return carry

    lax.fori_loop(0, layers * seqs, drain, 0)


def solution(mesh):
    rows_n, cols_n = mesh.shape['row'], mesh.shape['col']
    chips_n = rows_n // 2
    hidden_spec = P('rep', 'row')
    index_spec = P(('rep', 'row'))
    cache_spec = P(None, ('rep', 'row'), None, 'col', None)
    gain_spec = P(None, 'row')
    weight_spec = P(None, 'row', 'col')

    def device_program(h0, h1, pos, lens, cache_k, cache_v, gain_a, gain_m, wq, wk, wv, wo, wg, wu, wd):
        layers, seqs, ctx, heads, dim = cache_k.shape
        batch, ks = h0.shape
        hb, cb = batch // rows_n, batch // chips_n
        width = ks * rows_n
        cw, q_w, kv_w, ff = wo.shape[-1], wq.shape[-1], wk.shape[-1], wg.shape[-1]
        qkv_w = q_w + 2 * kv_w
        kc, vc = (jnp.transpose(x, (0, 1, 3, 4, 2)).reshape(layers, seqs, heads * dim, ctx) for x in (cache_k, cache_v))
        half = dim // 2
        table = ROPE_BASE ** (-(np.arange(128) % half) * 2.0 / dim)
        freq = jnp.asarray(table.reshape(1, 128), F32)
        vmem = pl.BlockSpec(memory_space=pltpu.VMEM)
        smem = pl.BlockSpec(memory_space=pltpu.SMEM)
        hbm = pl.BlockSpec(memory_space=pl.ANY)
        dma = pltpu.SemaphoreType.DMA

        def buf(*shape, dtype=BF16):
            return pltpu.VMEM(shape, dtype)

        ls = (layers, STEPS)
        ls1 = (layers + 1, STEPS)
        scratch = [
            buf(STEPS, batch, ks), buf(8, ks, dtype=F32), buf(8, width, dtype=F32),
            buf(layers, seqs, kv_w, ctx), buf(layers, seqs, kv_w, ctx),
            buf(layers, ks, qkv_w), buf(layers, ks, cw), buf(layers, 2 * ks, ff), buf(layers, *wd.shape[1:]),
            buf(*ls1, hb, width), buf(*ls, hb, width), buf(*ls1, hb, width), buf(*ls1, batch, ks),
            buf(*ls, batch, qkv_w), buf(*ls, rows_n - 1, hb, qkv_w),
            buf(*ls, hb, q_w), buf(*ls, batch, ks),
            buf(*ls, batch, cw), buf(*ls, rows_n - 1, hb, cw),
            buf(*ls, hb, width), buf(*ls, batch, 2 * ks),
            buf(*ls, batch, ff), buf(*ls, chips_n - 1, cb, ff),
            buf(*ls, cols_n, cb, ff // 2), buf(*ls, batch, ff // 2),
            buf(*ls, batch, cw), buf(*ls, rows_n - 1, hb, cw),
            buf(hb * 8, 128, dtype=F32), buf(hb * 8, 128, dtype=F32),
            buf(STEPS, hb, kv_w, dtype=F32), buf(STEPS, hb, kv_w, dtype=F32),
            buf(STEPS, hb, 128, dtype=F32), buf(STEPS, hb, 128, dtype=F32),
            dma((STEPS,)), dma((layers, 2)), dma((layers, 4)), dma((layers,)), dma((layers,)),
            dma((STEPS,)), dma((STEPS,)), dma(()), dma(()),
            dma(ls1), dma(ls1), dma(ls), dma(ls), dma(ls), dma(ls), dma(ls), dma(ls), dma(ls), dma(ls),
            dma(ls), dma(ls), dma(ls), dma(ls), dma(ls), dma((*ls, cols_n)), dma(ls), dma(ls), dma(ls), dma(ls),
            dma(ls), dma(ls), dma((STEPS,)),
        ]
        out_0, out_1, new_kv = pl.pallas_call(
            decode_kernel,
            out_shape=(jax.ShapeDtypeStruct(h0.shape, BF16), jax.ShapeDtypeStruct(h1.shape, BF16),
                       jax.ShapeDtypeStruct((layers, STEPS, 2, seqs, kv_w), F32)),
            in_specs=[hbm, hbm, smem, smem, hbm, hbm, vmem, vmem, vmem] + [hbm] * 7,
            out_specs=(hbm, hbm, vmem),
            scratch_shapes=scratch,
            compiler_params=pltpu.CompilerParams(collective_id=0, has_side_effects=True,
                                                 vmem_limit_bytes=58 * 1024 * 1024),
            name='decode',
        )(h0, h1, pos, lens, kc, vc, gain_a, gain_m, freq, wq, wk, wv, wo, wg, wu, wd)
        ko, vo = pl.pallas_call(
            cache_kernel,
            out_shape=(jax.ShapeDtypeStruct(kc.shape, BF16),) * 2,
            in_specs=[smem, vmem, hbm, hbm],
            out_specs=(hbm, hbm),
            scratch_shapes=[buf(2, layers * seqs, kv_w, ctx), dma((2, layers * seqs)), dma(())],
            compiler_params=pltpu.CompilerParams(vmem_limit_bytes=40 * 1024 * 1024),
            name='cache',
        )(lens, new_kv, kc, vc)
        ko, vo = (jnp.transpose(x.reshape(layers, seqs, heads, dim, ctx), (0, 1, 4, 2, 3)) for x in (ko, vo))
        return out_0, out_1, ko, vo

    return jax.shard_map(device_program, mesh=mesh,
                         in_specs=(hidden_spec, hidden_spec, index_spec, index_spec, cache_spec, cache_spec,
                                   gain_spec, gain_spec) + (weight_spec,) * 7,
                         out_specs=(hidden_spec, hidden_spec, cache_spec, cache_spec), check_vma=False)
```

time: 1170 us -> 176 us (0.15); the launches traced: 1160 us -> 176 us
  local copies, waits for them, and re-layouts: 354 us -> 5.49 us
  blocking collectives: 316 us -> 0 us
  waiting for transfers between devices: 298 us -> 0 us
  Pallas kernels: 0 us -> 170 us
  starting transfers between devices: 90.8 us -> 0 us
  matrix products: 58.9 us -> 0 us
  other arithmetic: 22.8 us -> 0 us
  between operations: 15 us -> 0.69 us
    reduce_scatter x16 -> x0, waiting for transfers between devices: 272 us -> none  [sum_rows(): lax.psum_scatter(partial.astype(jnp.bfloat16), 'row', scatter_dimension=0...]
    unnamed x66 -> x12, local copies, waits for them, and re-layouts: 200 us -> 5.49 us
    pallas_call x0 -> x2, Pallas kernels: none -> 170 us  [the longest x1 153 us: device_program(): pl.pallas_call(decode_kernel, out_shape=(jax.ShapeDtypeStruct(h0.shape, B...]
    all_gather x16 -> x0, blocking collectives: 155 us -> none  [to_row_features(): whole = lax.all_gather(block, 'col', axis=1, tiled=True)]
    scatter x10 -> x0, local copies, waits for them, and re-layouts: 98.3 us -> none  [the longest x5 49.2 us: decoder_layer(): cache_v = cache_v.at[layer, rows, slots].set(value_new)]
    all_to_all x10 -> x0, starting transfers between devices: 89.6 us -> none  [to_row_features(): return lax.all_to_all(whole, 'row', 1, 0, tiled=True)]
    all_to_all x6 -> x0, blocking collectives: 83.1 us -> none  [to_row_features(): return lax.all_to_all(whole, 'row', 1, 0, tiled=True)]
    psum x6 -> x0, blocking collectives: 77.4 us -> none  [rms_norm(): lax.psum(jnp.sum(hidden_f * hidden_f, axis=-1, keepdims=True), 'row')]
  transfers between devices with their start and end apart: 26 -> 0, of which waited for: 20 -> 0; matrix products, arithmetic and copies ran while one was open for 22% -> 0% of each run, Pallas kernels for 0% -> 0%
where the time goes in v1:
time: 176 us
  Pallas kernels  170 us (97%)
  local copies, waits for them, and re-layouts  5.49 us (3%)
    pallas_call x1, Pallas kernels, device_program(): pl.pallas_call(decode_kernel, out_shape=(jax.ShapeDtypeStruct(h0.shape, B...  153 us
    pallas_call x1, Pallas kernels, device_program(): pl.pallas_call(cache_kernel, out_shape=(jax.ShapeDtypeStruct(kc.shape, BF...  16.4 us
    unnamed x12, local copies, waits for them, and re-layouts  5.49 us

profile of v1, /device:TPU:97, one launch (start us, length us, event | category | flops | bytes accessed | tf_op | source)
XLA Modules:
  0.0 176.0 jit_solution(15087689137152224748)
XLA Ops:
  0.6 0.0 copy-start.2
  0.6 153.5 %decode.1 = (bf16[128,256]{1,0:T(8,128)(2,1)}, bf16[128,256]{1,0:T(8,128)(2,1)}, f32[2,2,2,16,128]{4,3,2,1,0:T(8,128)}) custom-call(bf16[128,256]{1,0:T(8,128)(2,1)} %h0.1, bf16[128,256]{1,0:T(8,128)(2,1)} %h1.1, s32[16]{0:T(128)} %pos.1, s32[16]{0:T(128)} %lens.3, bf16[2,16,128,1024]{3,2,1,0:T(8,128)(2,1)} %bitcast.12, bf16[2,16,128,1024]{3,2,1,0:T(8,128)(2,1)} %bitcast.14, ...), custom_call_target="tpu_custom_call" | custom-call | tf_op jit(solution)/shard_map/decode/pallas_call | solution.py:445
  154.1 0.0 copy-done.2
  154.1 0.0 copy-start
  154.1 3.4 %copy-done = bf16[2,16,1024,2,64]{2,4,3,1,0:T(8,128)(2,1)S(1)} copy-done((bf16[2,16,1024,2,64]{2,4,3,1,0:T(8,128)(2,1)S(1)}, bf16[2,16,1024,2,64]{2,4,3,1,0:T(8,128)(2,1)}, u32[]{:S(2)}) %copy-start) | copy-done | bytes 8388632
  157.5 0.0 copy-start.1
  157.5 0.8 copy-done.1
  158.4 0.0 copy-start.4
  158.4 0.0 copy-start.3
  158.4 16.4 %cache.1 = (bf16[2,16,128,1024]{3,2,1,0:T(8,128)(2,1)}, bf16[2,16,128,1024]{3,2,1,0:T(8,128)(2,1)}) custom-call(s32[16]{0:T(128)S(1)} %copy-done.2, f32[2,2,2,16,128]{4,3,2,1,0:T(8,128)S(1)} %copy-done.1, bf16[2,16,128,1024]{3,2,1,0:T(8,128)(2,1)S(1)} %bitcast.13, bf16[2,16,128,1024]{3,2,1,0:T(8,128)(2,1)} %bitcast.15), custom_call_target="tpu_custom_call" | custom-call | tf_op jit(solution)/shard_map/cache/pallas_call | solution.py:456
  174.7 0.0 copy-done.4
  174.8 0.6 copy.22
  175.4 0.0 copy-done.3
  175.4 0.6 copy.23
Async XLA Ops:
  0.6 153.5 %copy-start.2 = (s32[16]{0:T(128)S(1)}, s32[16]{0:T(128)}, u32[]{:S(2)}) copy-start(s32[16]{0:T(128)} %lens.3) | copy-start | bytes 196
  154.1 3.4 %copy-start = (bf16[2,16,1024,2,64]{2,4,3,1,0:T(8,128)(2,1)S(1)}, bf16[2,16,1024,2,64]{2,4,3,1,0:T(8,128)(2,1)}, u32[]{:S(2)}) copy-start(bf16[2,16,1024,2,64]{2,4,3,1,0:T(8,128)(2,1)} %param.20) | copy-start | bytes 25165828
  157.5 0.8 copy-start.1
  158.4 16.4 %copy-start.4 = (bf16[128,256]{1,0:T(8,128)(2,1)S(1)}, bf16[128,256]{1,0:T(8,128)(2,1)}, u32[]{:S(2)}) copy-start(bf16[128,256]{1,0:T(8,128)(2,1)} %get-tuple-element.18) | copy-start | bytes 196612
  158.4 17.0 %copy-start.3 = (bf16[128,256]{1,0:T(8,128)(2,1)S(1)}, bf16[128,256]{1,0:T(8,128)(2,1)}, u32[]{:S(2)}) copy-start(bf16[128,256]{1,0:T(8,128)(2,1)} %get-tuple-element.19) | copy-start | bytes 196612

commit v2 on v1

--- a/solution.py
+++ b/solution.py
@@ -14,6 +14,7 @@
 BF16 = jnp.bfloat16
 F32 = jnp.float32
 STEPS = 2
+CHUNKS = 4
 
 
 def at_multiple(index, size):
@@ -21,15 +22,15 @@
 
 
 def decode_kernel(
-        h0, h1, pos, lens, kc, vc, gain_a, gain_m, freq, wq, wk, wv, wo, wg, wu, wd,
-        out0, out1, new_kv,
-        hin, gsrc, gful, kbuf, vbuf, wqkv, wov, wgu, wdv,
+        h0, h1, pos_in, lens_in, kc, vc, gain_a_in, gain_m_in, freq_in, wq, wk, wv, wo, wg, wu, wd,
+        out0, out1, kbuf, vbuf,
+        hin, pos, lens, gain_a, gain_m, freq, gsrc, gful, sq, sqr, wqkv, wov, wgu, wdv,
         xst, xmid, nst1, nin1, qs, qr, ob, oin, os_, orr, nst2, nin2, gs, gr, aa, ab, ds_, dr,
         qf, of, kn, vn, cs, sn,
-        hin_sem, kv_sem, w_sem, wx_send, wx_recv, init_send, init_recv, g_send, g_recv,
+        hin_sem, small_sem, sq_send, sq_recv, kv_sem, w_sem, wx_send, wx_recv, init_send, init_recv, g_send, g_recv,
         n1_send, n1_recv, q_send, q_recv, o_send, o_recv, ro_send, ro_recv, x_send, x_recv,
         n2_send, n2_recv, gu_send, gu_recv, aa_send, aa_recv, ab_send, ab_recv, rd_send, rd_recv,
-        x2_send, x2_recv, out_sem):
+        x2_send, x2_recv):
     layers = wq.shape[0]
     rows_n = lax.axis_size('row')
     cols_n = lax.axis_size('col')
@@ -47,6 +48,7 @@
     ff = wg.shape[-1]
     fh = ff // 2
     cb = batch // chips_n
+    fc = fh // CHUNKS
     ctx = kc.shape[-1]
     hins = (h0, h1)
     outs = (out0, out1)
@@ -62,21 +64,25 @@
     def wait_send(ref, sem):
         peer_copy(ref, ref, sem, sem, r, c).wait_send()
 
+    def gate_up(l, k, half):
+        columns = pl.ds(pl.multiple_of(half * fh + k // 2 * fc, fc), fc)
+        return (wg, wu)[k % 2].at[l, :, columns], wgu.at[l, at_multiple(core, ks), pl.ds(k * fc, fc)]
+
+    small = [pltpu.make_async_copy(src, dst, small_sem.at[k]) for k, (src, dst) in enumerate(
+        ((gain_a_in, gain_a), (gain_m_in, gain_m), (freq_in, freq), (pos_in, pos), (lens_in, lens)))]
     for s in range(STEPS):
         pltpu.make_async_copy(hins[s], hin.at[s], hin_sem.at[s]).start()
+    for copy in small:
+        copy.start()
     for l in range(layers):
         for src, lo, n in ((wq, 0, q_w), (wk, q_w, kv_w), (wv, q_w + kv_w, kv_w)):
             pltpu.make_async_copy(src.at[l], wqkv.at[l, :, pl.ds(lo, n)], w_sem.at[l, 0]).start()
         pltpu.make_async_copy(kc.at[l], kbuf.at[l], kv_sem.at[l, 0]).start()
         pltpu.make_async_copy(vc.at[l], vbuf.at[l], kv_sem.at[l, 1]).start()
         pltpu.make_async_copy(wo.at[l], wov.at[l], w_sem.at[l, 1]).start()
-        for k, src in enumerate((wg, wu)):
-            pltpu.make_async_copy(src.at[l, :, at_multiple(core, fh)],
-                                  wgu.at[l, at_multiple(core, ks), pl.ds(k * fh, fh)], w_sem.at[l, 2]).start()
+        for k in range(2 * CHUNKS):
+            pltpu.make_async_copy(*gate_up(l, k, core), w_sem.at[l, 2]).start()
         pltpu.make_async_copy(wd.at[l], wdv.at[l], w_sem.at[l, 3]).start()
-    gsrc[...] = jnp.concatenate([gain_a[...].astype(F32), gain_m[...].astype(F32),
-                                 jnp.zeros((gsrc.shape[0] - 2 * layers, ks), F32)], axis=0)
-    gful[:, at_multiple(r, ks)] = gsrc[...]
 
     barrier = pltpu.get_barrier_semaphore()
     for k in range(1, rows_n * cols_n):
@@ -88,19 +94,30 @@
     def row_peer(d):
         return lax.rem(r + d, rows_n)
 
-    for d in range(1, rows_n):
-        peer_copy(gsrc, gful.at[:, at_multiple(r, ks)], g_send, g_recv, row_peer(d), c).start()
+    def row_sums(s):
+        xf = hin[s].astype(F32)
+        return jnp.sum(xf * xf, axis=-1, keepdims=True)
+
     for s in range(STEPS):
         pltpu.make_async_copy(hins[s], hin.at[s], hin_sem.at[s]).wait()
+        sq[s] = jnp.transpose(jnp.broadcast_to(row_sums(s), (batch, batch)))[:8]
+        for d in range(1, rows_n):
+            peer_copy(sq.at[s], sqr.at[s, d - 1], sq_send.at[s], sq_recv.at[s], row_peer(d), c).start()
+    for s in range(STEPS):
         for d in range(1, rows_n):
             peer_copy(hin.at[s, at_multiple(row_peer(d), hb), :], xst.at[0, s, :, at_multiple(r, ks)],
                       init_send.at[s], init_recv.at[s], row_peer(d), c).start()
         xst[0, s, :, at_multiple(r, ks)] = hin[s, at_multiple(r, hb), :]
+    for copy in small:
+        copy.wait()
+    gsrc[...] = jnp.concatenate([gain_a[...].astype(F32), gain_m[...].astype(F32),
+                                 jnp.zeros((gsrc.shape[0] - 2 * layers, ks), F32)], axis=0)
+    gful[:, at_multiple(r, ks)] = gsrc[...]
+    for d in range(1, rows_n):
+        peer_copy(gsrc, gful.at[:, at_multiple(r, ks)], g_send, g_recv, row_peer(d), c).start()
     for l in range(layers):
-        for k, src in enumerate((wg, wu)):
-            peer_copy(src.at[l, :, at_multiple(1 - core, fh)],
-                      wgu.at[l, at_multiple(core, ks), pl.ds(k * fh, fh)],
-                      wx_send.at[l], wx_recv.at[l], r + 1 - 2 * core, c).start()
+        for k in range(2 * CHUNKS):
+            peer_copy(*gate_up(l, k, 1 - core), wx_send.at[l], wx_recv.at[l], r + 1 - 2 * core, c).start()
 
     lane = lax.broadcasted_iota(jnp.int32, (hb, 128), 1)
     sub = lax.broadcasted_iota(jnp.int32, (hb, 128), 0)
@@ -125,11 +142,14 @@
                       n1_send.at[l, s], n1_recv.at[l, s], row_peer(d), c).start()
         nin1[l, s, at_multiple(r, hb), :] = nst1[l, s, :, at_multiple(r, ks)]
 
-    wait_recv(gful.at[:, pl.ds(0, (rows_n - 1) * ks)], g_recv)
-    for s in range(STEPS):
-        wait_recv(xst.at[0, s, :, pl.ds(0, (rows_n - 1) * ks)], init_recv.at[s])
-        nst1[0, s] = norm_rows(xst[0, s], 0)
-        send_n1(0, s)
+    for s in range(STEPS):
+        wait_recv(sqr.at[s], sq_recv.at[s])
+        total = sq[s]
+        for d in range(rows_n - 1):
+            total += sqr[s, d]
+        total = jnp.transpose(jnp.broadcast_to(total[:1], (batch, batch)))[:, :1]
+        scale = lax.rsqrt(total * (1.0 / width) + EPS)
+        nin1[0, s] = (hin[s].astype(F32) * scale * gain_a[:1, :].astype(F32)).astype(BF16)
 
     def reduce_rows(stage, recv, sem, l, s):
         wait_recv(recv.at[l, s], sem.at[l, s])
@@ -153,8 +173,6 @@
         val = qkv[:, q_w + kv_w:]
         kn[s] = key
         vn[s] = val
-        new_kv[l, s, 0] = key
-        new_kv[l, s, 1] = val
         for t in range(4):
             kv, pair = t // 2, t % 2
             y = rope(qkv[:, 128 * t:128 * t + 128], s)
@@ -209,6 +227,24 @@
                 else:
                     copy.start()
 
+    def insert_new(l):
+        sub8 = lax.broadcasted_iota(jnp.int32, (8, kv_w), 0)
+        slot = lax.broadcasted_iota(jnp.int32, (8, ctx), 1)
+        step = lax.broadcasted_iota(jnp.int32, (8, ctx), 0)
+        wide = lax.broadcasted_iota(jnp.int32, (kv_w, ctx), 1)
+
+        def one(b, carry):
+            first = lens[b]
+            at = jnp.where((step < STEPS) & (slot == first + step), 1.0, 0.0).astype(BF16)
+            fresh = (wide >= first) & (wide < first + STEPS)
+            for new, cache in ((kn, kbuf), (vn, vbuf)):
+                rows = jnp.where(sub8 == 0, new[0, pl.ds(b, 1), :], jnp.where(sub8 == 1, new[1, pl.ds(b, 1), :], 0.0))
+                spread = lax.dot_general(rows.astype(BF16), at, (((0,), (0,)), ((), ())), preferred_element_type=F32)
+                cache[l, b] = jnp.where(fresh, spread, cache[l, b].astype(F32)).astype(BF16)
+            return carry
+
+        lax.fori_loop(0, hb, one, 0)
+
     def on_own_column(full, short, wait, sem):
         @pl.when(chip == c)
         def _():
@@ -233,7 +269,10 @@
             if s == 0:
                 for src, lo, n in ((wq, 0, q_w), (wk, q_w, kv_w), (wv, q_w + kv_w, kv_w)):
                     pltpu.make_async_copy(src.at[l], wqkv.at[l, :, pl.ds(lo, n)], w_sem.at[l, 0]).wait()
-            wait_recv(nin1.at[l, s, pl.ds(0, batch - hb), :], n1_recv.at[l, s])
+            @pl.when(l > 0)
+            def _():
+                wait_recv(nin1.at[l, s, pl.ds(0, batch - hb), :], n1_recv.at[l, s])
+
             qs[l, s] = jnp.dot(nin1[l, s], wqkv[l], preferred_element_type=F32).astype(BF16)
             scatter_rows(qs, qr, q_send, q_recv, l, s)
         for s in range(STEPS):
@@ -248,9 +287,18 @@
             os_[l, s] = jnp.dot(oin[l, s], wov[l], preferred_element_type=F32).astype(BF16)
             scatter_rows(os_, orr, ro_send, ro_recv, l, s)
         for s in range(STEPS):
+            @pl.when(l == 0)
+            def _():
+                wait_recv(xst.at[0, s, :, pl.ds(0, (rows_n - 1) * ks)], init_recv.at[s])
+
             total = reduce_rows(os_, orr, ro_recv, l, s)
             gather_cols(xmid.at[l, s], add_block(xst.at[l, s], total), x_send.at[l, s], x_recv.at[l, s])
         for s in range(STEPS):
+            if s == 0:
+                @pl.when(l == 0)
+                def _():
+                    wait_recv(gful.at[:, pl.ds(0, (rows_n - 1) * ks)], g_recv)
+
             wait_recv(xmid.at[l, s, :, pl.ds(0, width - cw)], x_recv.at[l, s])
             nst2[l, s] = norm_rows(xmid[l, s], layers + l)
             for d in range(1, rows_n):
@@ -260,47 +308,55 @@
             nin2[l, s, at_multiple(r, hb), :] = nst2[l, s, :, at_multiple(chip, 2 * ks)]
         for s in range(STEPS):
             if s == 0:
-                for k, src in enumerate((wg, wu)):
-                    pltpu.make_async_copy(src.at[l, :, at_multiple(core, fh)],
-                                          wgu.at[l, at_multiple(core, ks), pl.ds(k * fh, fh)], w_sem.at[l, 2]).wait()
+                for k in range(2 * CHUNKS):
+                    pltpu.make_async_copy(*gate_up(l, k, core), w_sem.at[l, 2]).wait()
                 wait_recv(wgu.at[l, pl.ds(0, ks), :], wx_recv.at[l])
             wait_recv(nin2.at[l, s, pl.ds(0, batch - hb), :], n2_recv.at[l, s])
-            tile = 512
-
-            def columns(k, carry):
-                gs[l, s, :, at_multiple(k, tile)] = jnp.dot(
-                    nin2[l, s], wgu[l, :, at_multiple(k, tile)], preferred_element_type=F32).astype(BF16)
-                return carry
-
-            lax.fori_loop(0, 2 * fh // tile, columns, 0)
-            for d in range(1, chips_n):
-                to = lax.rem(chip + d, chips_n)
-                peer_copy(gs.at[l, s, at_multiple(to, cb), :], gr.at[l, s, d - 1],
-                          gu_send.at[l, s], gu_recv.at[l, s], 2 * to + core, c).start()
-        for s in range(STEPS):
-            wait_recv(gr.at[l, s], gu_recv.at[l, s])
-            total = gs[l, s, at_multiple(chip, cb), :].astype(F32)
+            for k in range(CHUNKS):
+                columns = pl.ds(k * 2 * fc, 2 * fc)
+                gs[l, s, :, columns] = jnp.dot(nin2[l, s], wgu[l, :, columns], preferred_element_type=F32).astype(BF16)
+                for d in range(1, chips_n):
+                    to = lax.rem(chip + d, chips_n)
+                    peer_copy(gs.at[l, s, at_multiple(to, cb), columns], gr.at[l, s, d - 1, :, columns],
+                              gu_send.at[l, s], gu_recv.at[l, s, k], 2 * to + core, c).start()
+        insert_new(l)
+
+        def activate(s, k):
+            columns = pl.ds(k * 2 * fc, 2 * fc)
+            wait_recv(gr.at[l, s, :, :, columns], gu_recv.at[l, s, k])
+            total = gs[l, s, at_multiple(chip, cb), columns].astype(F32)
             for d in range(chips_n - 1):
-                total += gr[l, s, d].astype(F32)
+                total += gr[l, s, d, :, columns].astype(F32)
             total = total.astype(BF16).astype(F32)
-            gate, up = total[:, :fh], total[:, fh:]
-            aa[l, s, c] = (gate / (1.0 + jnp.exp(-gate)) * up).astype(BF16)
+            gate, up = total[:, :fc], total[:, fc:]
+            part = pl.ds(k * fc, fc)
+            aa[l, s, c, :, part] = (gate / (1.0 + jnp.exp(-gate)) * up).astype(BF16)
             for d in range(1, cols_n):
-                peer_copy(aa.at[l, s, c], aa.at[l, s, c], aa_send.at[l, s], aa_recv.at[l, s, c],
+                peer_copy(aa.at[l, s, c, :, part], aa.at[l, s, c, :, part], aa_send.at[l, s], aa_recv.at[l, s, k, c],
                           r, lax.rem(c + d, cols_n)).start()
-        for s in range(STEPS):
+
+        def relay(s, k):
+            part = pl.ds(k * fc, fc)
             for d in (1, 2, 3, 0):
                 to = lax.rem(chip + d, chips_n)
 
                 @pl.when(to != c)
                 def _():
-                    wait_recv(aa.at[l, s, to], aa_recv.at[l, s, to])
+                    wait_recv(aa.at[l, s, to, :, part], aa_recv.at[l, s, k, to])
 
                 if d:
-                    peer_copy(aa.at[l, s, to], ab.at[l, s, at_multiple(chip, cb), :],
+                    peer_copy(aa.at[l, s, to, :, part], ab.at[l, s, at_multiple(chip, cb), part],
                               ab_send.at[l, s], ab_recv.at[l, s], 2 * to + core, c).start()
                 else:
-                    ab[l, s, at_multiple(chip, cb), :] = aa[l, s, to]
+                    ab[l, s, at_multiple(chip, cb), part] = aa[l, s, to, :, part]
+
+        work = [(s, k) for s in range(STEPS) for k in range(CHUNKS)]
+        lag = 2
+        for t in range(len(work) + lag):
+            if t < len(work):
+                activate(*work[t])
+            if t >= lag:
+                relay(*work[t - lag])
         for s in range(STEPS):
             if s == 0:
                 pltpu.make_async_copy(wd.at[l], wdv.at[l], w_sem.at[l, 3]).wait()
@@ -322,17 +378,18 @@
 
     for s in range(STEPS):
         wait_recv(nin1.at[layers, s, pl.ds(0, batch - hb), :], n1_recv.at[layers, s])
-        pltpu.make_async_copy(nin1.at[layers, s], outs[s], out_sem.at[s]).start()
+        outs[s][...] = nin1[layers, s]
 
     for d in range(1, rows_n):
         wait_send(gsrc, g_send)
     for s in range(STEPS):
+        wait_send(sqr.at[s], sq_send.at[s])
         wait_send(hin.at[s, pl.ds(0, batch - hb), :], init_send.at[s])
 
     def finish(l, carry):
         wait_send(wgu.at[l, pl.ds(0, ks), :], wx_send.at[l])
         for s in range(STEPS):
-            wait_send(nin1.at[l, s, pl.ds(0, batch - hb), :], n1_send.at[l, s])
+            wait_send(nin1.at[l + 1, s, pl.ds(0, batch - hb), :], n1_send.at[l + 1, s])
             wait_send(qr.at[l, s], q_send.at[l, s])
             on_own_column(oin.at[l, s], oin.at[l, s, pl.ds(0, batch - hb), :], wait_send, o_send.at[l, s])
             wait_send(orr.at[l, s], ro_send.at[l, s])
@@ -346,49 +403,6 @@
         return carry
 
     lax.fori_loop(0, layers, finish, 0)
-    for s in range(STEPS):
-        wait_send(nin1.at[layers, s, pl.ds(0, batch - hb), :], n1_send.at[layers, s])
-        pltpu.make_async_copy(nin1.at[layers, s], outs[s], out_sem.at[s]).wait()
-
-
-def cache_kernel(lens, new_kv, kc, vc, ko, vo, buf, in_sem, out_sem):
-    layers, seqs = kc.shape[0], kc.shape[1]
-    caches, results = (kc, vc), (ko, vo)
-
-    def load(i, carry):
-        l, b = i // seqs, lax.rem(i, seqs)
-        for w in range(2):
-            pltpu.make_async_copy(caches[w].at[l, b], buf.at[w, i], in_sem.at[w, i]).start()
-        return carry
-
-    def store(i, carry):
-        l, b = i // seqs, lax.rem(i, seqs)
-        first = lens[b]
-        rows = lax.broadcasted_iota(jnp.int32, (8, 128), 0)
-        lane = lax.broadcasted_iota(jnp.int32, (kc.shape[2], 128), 1)
-        for w in range(2):
-            pltpu.make_async_copy(caches[w].at[l, b], buf.at[w, i], in_sem.at[w, i]).wait()
-            for s in range(STEPS):
-                row = jnp.broadcast_to(new_kv[l, s, w, pl.ds(b, 1), :], (8, 128))
-                spread = lax.dot_general(jnp.where(rows == 0, row, 0.0).astype(BF16), jnp.ones((8, 128), BF16),
-                                         (((0,), (0,)), ((), ())), preferred_element_type=F32)
-                slot = first + s
-                window = pl.ds(pl.multiple_of(slot // 128 * 128, 128), 128)
-                old = buf[w, i, :, window].astype(F32)
-                buf[w, i, :, window] = jnp.where(lane == lax.rem(slot, 128), spread, old).astype(BF16)
-            pltpu.make_async_copy(buf.at[w, i], results[w].at[l, b], out_sem).start()
-        return carry
-
-    lax.fori_loop(0, layers * seqs, load, 0)
-    lax.fori_loop(0, layers * seqs, store, 0)
-
-    def drain(i, carry):
-        l, b = i // seqs, lax.rem(i, seqs)
-        for w in range(2):
-            pltpu.make_async_copy(buf.at[w, i], results[w].at[l, b], out_sem).wait()
-        return carry
-
-    lax.fori_loop(0, layers * seqs, drain, 0)
 
 
 def solution(mesh):
@@ -412,8 +426,7 @@
         table = ROPE_BASE ** (-(np.arange(128) % half) * 2.0 / dim)
         freq = jnp.asarray(table.reshape(1, 128), F32)
         vmem = pl.BlockSpec(memory_space=pltpu.VMEM)
-        smem = pl.BlockSpec(memory_space=pltpu.SMEM)
-        hbm = pl.BlockSpec(memory_space=pl.ANY)
+        hbm = pl.BlockSpec(memory_space=pltpu.HBM)
         dma = pltpu.SemaphoreType.DMA
 
         def buf(*shape, dtype=BF16):
@@ -422,8 +435,9 @@
         ls = (layers, STEPS)
         ls1 = (layers + 1, STEPS)
         scratch = [
-            buf(STEPS, batch, ks), buf(8, ks, dtype=F32), buf(8, width, dtype=F32),
-            buf(layers, seqs, kv_w, ctx), buf(layers, seqs, kv_w, ctx),
+            buf(STEPS, batch, ks), pltpu.SMEM(pos.shape, pos.dtype), pltpu.SMEM(lens.shape, lens.dtype),
+            buf(*gain_a.shape), buf(*gain_m.shape), buf(1, 128, dtype=F32), buf(8, ks, dtype=F32), buf(8, width, dtype=F32),
+            buf(STEPS, 8, batch, dtype=F32), buf(STEPS, rows_n - 1, 8, batch, dtype=F32),
             buf(layers, ks, qkv_w), buf(layers, ks, cw), buf(layers, 2 * ks, ff), buf(layers, *wd.shape[1:]),
             buf(*ls1, hb, width), buf(*ls, hb, width), buf(*ls1, hb, width), buf(*ls1, batch, ks),
             buf(*ls, batch, qkv_w), buf(*ls, rows_n - 1, hb, qkv_w),
@@ -436,32 +450,24 @@
             buf(hb * 8, 128, dtype=F32), buf(hb * 8, 128, dtype=F32),
             buf(STEPS, hb, kv_w, dtype=F32), buf(STEPS, hb, kv_w, dtype=F32),
             buf(STEPS, hb, 128, dtype=F32), buf(STEPS, hb, 128, dtype=F32),
-            dma((STEPS,)), dma((layers, 2)), dma((layers, 4)), dma((layers,)), dma((layers,)),
+            dma((STEPS,)), dma((5,)), dma((STEPS,)), dma((STEPS,)), dma((layers, 2)), dma((layers, 4)), dma((layers,)), dma((layers,)),
             dma((STEPS,)), dma((STEPS,)), dma(()), dma(()),
             dma(ls1), dma(ls1), dma(ls), dma(ls), dma(ls), dma(ls), dma(ls), dma(ls), dma(ls), dma(ls),
-            dma(ls), dma(ls), dma(ls), dma(ls), dma(ls), dma((*ls, cols_n)), dma(ls), dma(ls), dma(ls), dma(ls),
-            dma(ls), dma(ls), dma((STEPS,)),
+            dma(ls), dma(ls), dma(ls), dma((*ls, CHUNKS)), dma(ls), dma((*ls, CHUNKS, cols_n)), dma(ls), dma(ls), dma(ls), dma(ls),
+            dma(ls), dma(ls),
         ]
-        out_0, out_1, new_kv = pl.pallas_call(
+        out_0, out_1, ko, vo = pl.pallas_call(
             decode_kernel,
-            out_shape=(jax.ShapeDtypeStruct(h0.shape, BF16), jax.ShapeDtypeStruct(h1.shape, BF16),
-                       jax.ShapeDtypeStruct((layers, STEPS, 2, seqs, kv_w), F32)),
-            in_specs=[hbm, hbm, smem, smem, hbm, hbm, vmem, vmem, vmem] + [hbm] * 7,
-            out_specs=(hbm, hbm, vmem),
+            out_shape=(pltpu.VMEM(h0.shape, BF16), pltpu.VMEM(h1.shape, BF16),
+                       pltpu.VMEM(kc.shape, BF16), pltpu.VMEM(vc.shape, BF16)),
+            in_specs=[hbm] * 16,
+            out_specs=(vmem,) * 4,
             scratch_shapes=scratch,
             compiler_params=pltpu.CompilerParams(collective_id=0, has_side_effects=True,
-                                                 vmem_limit_bytes=58 * 1024 * 1024),
+                                                 vmem_limit_bytes=36 * 1024 * 1024),
             name='decode',
-        )(h0, h1, pos, lens, kc, vc, gain_a, gain_m, freq, wq, wk, wv, wo, wg, wu, wd)
-        ko, vo = pl.pallas_call(
-            cache_kernel,
-            out_shape=(jax.ShapeDtypeStruct(kc.shape, BF16),) * 2,
-            in_specs=[smem, vmem, hbm, hbm],
-            out_specs=(hbm, hbm),
-            scratch_shapes=[buf(2, layers * seqs, kv_w, ctx), dma((2, layers * seqs)), dma(())],
-            compiler_params=pltpu.CompilerParams(vmem_limit_bytes=40 * 1024 * 1024),
-            name='cache',
-        )(lens, new_kv, kc, vc)
+        )(*(pltpu.with_memory_space_constraint(x, pltpu.HBM)
+            for x in (h0, h1, pos, lens, kc, vc, gain_a, gain_m, freq, wq, wk, wv, wo, wg, wu, wd)))
         ko, vo = (jnp.transpose(x.reshape(layers, seqs, heads, dim, ctx), (0, 1, 4, 2, 3)) for x in (ko, vo))
         return out_0, out_1, ko, vo
 

time: 176 us -> 160 us (0.909)
  Pallas kernels: 170 us -> 151 us
  local copies, waits for them, and re-layouts: 5.49 us -> 8.05 us
    pallas_call x2 -> x1, Pallas kernels: 170 us -> 151 us  [device_program(): pl.pallas_call(decode_kernel, out_shape=(pltpu.VMEM(h0.shape, BF16), pltp...]
    unnamed x12 -> x4, local copies, waits for them, and re-layouts: 5.49 us -> 8.05 us
where the time goes in v2:
time: 160 us
  Pallas kernels  151 us (94%)
  local copies, waits for them, and re-layouts  8.05 us (5%)
    pallas_call x1, Pallas kernels, device_program(): pl.pallas_call(decode_kernel, out_shape=(pltpu.VMEM(h0.shape, BF16), pltp...  151 us
    unnamed x4, local copies, waits for them, and re-layouts  8.05 us

profile of v2, /device:TPU:97, one launch (start us, length us, event | category | flops | bytes accessed | tf_op | source)
XLA Modules:
  0.0 160.0 jit_solution(1917964549871394986)
XLA Ops:
  0.6 151.3 %decode.1 = (bf16[128,256]{1,0:T(8,128)(2,1)S(1)}, bf16[128,256]{1,0:T(8,128)(2,1)S(1)}, bf16[2,16,128,1024]{3,2,1,0:T(8,128)(2,1)S(1)}, bf16[2,16,128,1024]{3,2,1,0:T(8,128)(2,1)S(1)}) custom-call(bf16[128,256]{1,0:T(8,128)(2,1)} %h0.1, bf16[128,256]{1,0:T(8,128)(2,1)} %h1.1, s32[16]{0:T(128)} %pos_in.1, s32[16]{0:T(128)} %lens_in.1, ...), custom_call_target="tpu_custom_call" | custom-call | tf_op jit(solution)/shard_map/decode/pallas_call | solution.py:459
  152.0 0.6 copy.24
  152.6 0.6 copy.25
  153.2 3.4 %copy.26 = bf16[2,16,1024,2,64]{2,4,3,1,0:T(8,128)(2,1)} copy(bf16[2,16,1024,2,64]{2,4,3,1,0:T(8,128)(2,1)S(1)} %bitcast.13) | data formatting | bytes 16777216
  156.6 3.4 %copy.27 = bf16[2,16,1024,2,64]{2,4,3,1,0:T(8,128)(2,1)} copy(bf16[2,16,1024,2,64]{2,4,3,1,0:T(8,128)(2,1)S(1)} %bitcast.12) | data formatting | bytes 16777216
